TPU v7x, 32 devices: a whole 2x2x4 slice. The times are simulated.
32 devices in a mesh: panel: 4 (over z), rows: 8 (over y, x, core).
Axes of the slice: x: 2, y: 2, z: 4, core: 2. Of those that a mesh axis runs over, the one named last changes fastest.
Arguments:
- rhs_diag: bfloat16 [4, 4096, 128], P(None, 'rows'), may hold values from -6 to 6
- rhs_tall: bfloat16 [4, 4096, 128], P('panel', 'rows'), may hold values from -6 to 6
- diag_inverse: bfloat16 [4, 1024, 1024], P('panel'), may hold values from -0.1875 to 0.1875
- coupling: bfloat16 [4, 4096, 1024], P('panel', 'rows'), may hold values from -0.09375 to 0.09375
- tall_blocks: bfloat16 [4, 32, 128, 1024], P('panel', 'rows'), may hold values from -0.125 to 0.125
- sparsity: int32 [32, 4], P('rows', 'panel'), may hold values 0 or 1
Outputs:
- solution: float32 [4, 4, 1024, 128], P('panel', None, 'rows')
- tall_residual: float32 [4, 4096, 128], P('panel', 'rows')
All inputs are finite; a program needn't handle non-finite values. No bound on the sum of `sparsity` on one device may be relied on, other than what follows from the above.
Results may differ from a plain program's by a relative error of at most 0.0085.
Values may be sent and summed in bfloat16 or wider, within the bound.
A program may use at most 64 MiB of HBM per device.

v0:
```python
import jax
import jax.numpy as jnp
from jax import lax
from jax.sharding import PartitionSpec as P


def shifted(block, axis, distance):
    devices = range(lax.axis_size(axis))
    route = [(i - distance, i) for i in devices if i - distance in devices]
    return lax.ppermute(block, axis, route)


def per_device(rhs_diag, rhs_tall, diag_inverse, coupling, tall_blocks, sparsity):
    panel_index = lax.axis_index("panel")
    rows_index = lax.axis_index("rows")
    panel_count = lax.axis_size("panel")
    rows_count = lax.axis_size("rows")
    batches, rows_here, columns = rhs_diag.shape
    panel_width = diag_inverse.shape[1]
    slice_rows = panel_width // rows_count
    blocks_here = tall_blocks.shape[1]
    block_rows = tall_blocks.shape[2]
    tall_rows = blocks_here * block_rows
    rows_panel = rows_index * rows_here // panel_width
    offset = jnp.clip(
        rows_index * rows_here - panel_index * panel_width, 0, panel_width - rows_here
    )
    inverse_cols = lax.dynamic_slice_in_dim(diag_inverse[0], offset, rows_here, 1)
    owner = rows_panel == panel_index
    is_later = rows_panel > panel_index
    coupling_here = coupling[0]
    tall_matrix = tall_blocks[0].reshape(tall_rows, panel_width)
    block_mask = jnp.repeat(sparsity[:, 0].astype(jnp.float32), block_rows)[:, None]

    def advance(tick_number, state_now):
        incoming, solutions, stored = state_now
        batch_now = tick_number - panel_index
        active = (batch_now >= 0) & (batch_now < batches)
        batch_safe = jnp.clip(batch_now, 0, batches - 1)
        rhs_now = lax.dynamic_index_in_dim(rhs_diag, batch_safe, 0, keepdims=False).astype(
            jnp.float32
        )
        reduced = (rhs_now - incoming).astype(jnp.bfloat16)
        partial_value = jnp.dot(inverse_cols, reduced, preferred_element_type=jnp.float32)
        partial_value = jnp.where(owner, partial_value, jnp.float32(0.0))
        own_rows = lax.psum_scatter(partial_value, "rows", scatter_dimension=0, tiled=True)
        solved = lax.all_gather(own_rows.astype(jnp.bfloat16), "rows", axis=0, tiled=True)
        previous = lax.dynamic_index_in_dim(solutions, batch_safe, 0, keepdims=False)
        solutions = lax.dynamic_update_index_in_dim(
            solutions, jnp.where(active, own_rows, previous), batch_safe, 0
        )
        update = jnp.dot(coupling_here, solved, preferred_element_type=jnp.float32)
        outgoing = incoming + jnp.where(is_later, update, jnp.float32(0.0))
        earlier = lax.dynamic_index_in_dim(stored, batch_safe, 0, keepdims=False)
        stored = lax.dynamic_update_index_in_dim(
            stored, jnp.where(active, solved, earlier), batch_safe, 0
        )
        incoming = shifted(outgoing, "panel", 1)
        return (incoming, solutions, stored)

    stored = jnp.zeros((batches, panel_width, columns), jnp.bfloat16)
    initial = (
        jnp.zeros((rows_here, columns), jnp.float32),
        jnp.zeros((batches, slice_rows, columns), jnp.float32),
        stored,
    )
    tick_count = batches + panel_count - 1
    incoming, solutions, stored = lax.fori_loop(0, tick_count, advance, initial)
    tall_terms = (
        jnp.einsum("rw,bws->brs", tall_matrix, stored, preferred_element_type=jnp.float32)
        * block_mask
    )
    summed = lax.psum_scatter(tall_terms, "panel", scatter_dimension=0, tiled=True)
    tall_residual = rhs_tall.astype(jnp.float32) - summed
    return (solutions[None], tall_residual)


def solution(mesh):
    placed = (
        P(None, "rows", None),
        P("panel", "rows", None),
        P("panel", None, None),
        P("panel", "rows", None),
        P("panel", "rows", None, None),
        P("rows", "panel"),
    )
    return jax.shard_map(
        per_device,
        mesh=mesh,
        in_specs=placed,
        out_specs=(P("panel", None, "rows", None), P("panel", "rows", None)),
        check_vma=False,
    )
```

profile of v0, /device:TPU:17, one launch (start us, length us, event | category | flops | bytes accessed | tf_op | source)
XLA Modules:
  0.0 481.5 jit_solution(7875205696429187372)
XLA Ops:
  12.7 430.4 %while.17 = (s32[]{:T(128)}, f32[512,128]{0,1:T(8,128)}, f32[4,128,128]{2,1,0:T(8,128)}, bf16[4,1024,128]{1,2,0:T(8,128)(2,1)}, pred[]{:T(512)}, /*index=5*/pred...) while((s32[]{:T(128)}, f32[512,128]{0,1:T(8,128)}, ...), condition=%wide.region_2.3_spmd, body=%wide.region_0.2_spmd.sunk | while | flops 269058048 | bytes 9503014 | solution.py:68
  18.6 32.6 %reduce-scatter.5.cloned.1.call-done = f32[128,128]{0,1:T(8,128)} async-done(((f32[1024,128]{0,1:T(8,128)}), f32[128,128]{0,1:T(8,128)}) %reduce-scatter.5.cloned.1.call-update) | async-done | bytes 65552 | tf_op jit(solution)/shard_map/while/body/eval_jaxpr/reduce_scatter | solution.py:46
  52.1 10.4 %all_gather.8 = bf16[1024,128]{0,1:T(8,128)(2,1)S(1)} all-gather(bf16[128,128]{0,1:T(8,128)(2,1)S(1)} %get-tuple-element.271), channel_id=1, replica_groups=mesh['panel'=4,'rows'=8] {'rows'}, dimensions={0}, use_global_device_ids=true | all-gather | bytes 294912 | tf_op jit(solution)/shard_map/while/body/eval_jaxpr/all_gather | solution.py:47
  70.5 4.3 collective-permute-done
  80.8 31.9 %reduce-scatter.5.cloned.1.call-done = f32[128,128]{0,1:T(8,128)} async-done(((f32[1024,128]{0,1:T(8,128)}), f32[128,128]{0,1:T(8,128)}) %reduce-scatter.5.cloned.1.call-update) | async-done | bytes 65552 | tf_op jit(solution)/shard_map/while/body/eval_jaxpr/reduce_scatter | solution.py:46
  113.6 10.4 %all_gather.8 = bf16[1024,128]{0,1:T(8,128)(2,1)S(1)} all-gather(bf16[128,128]{0,1:T(8,128)(2,1)S(1)} %get-tuple-element.271), channel_id=1, replica_groups=mesh['panel'=4,'rows'=8] {'rows'}, dimensions={0}, use_global_device_ids=true | all-gather | bytes 294912 | tf_op jit(solution)/shard_map/while/body/eval_jaxpr/all_gather | solution.py:47
  132.1 4.3 collective-permute-done
  142.3 31.9 %reduce-scatter.5.cloned.1.call-done = f32[128,128]{0,1:T(8,128)} async-done(((f32[1024,128]{0,1:T(8,128)}), f32[128,128]{0,1:T(8,128)}) %reduce-scatter.5.cloned.1.call-update) | async-done | bytes 65552 | tf_op jit(solution)/shard_map/while/body/eval_jaxpr/reduce_scatter | solution.py:46
  175.1 10.4 %all_gather.8 = bf16[1024,128]{0,1:T(8,128)(2,1)S(1)} all-gather(bf16[128,128]{0,1:T(8,128)(2,1)S(1)} %get-tuple-element.271), channel_id=1, replica_groups=mesh['panel'=4,'rows'=8] {'rows'}, dimensions={0}, use_global_device_ids=true | all-gather | bytes 294912 | tf_op jit(solution)/shard_map/while/body/eval_jaxpr/all_gather | solution.py:47
  193.6 4.3 collective-permute-done
  203.8 31.6 %reduce-scatter.5.cloned.1.call-done = f32[128,128]{0,1:T(8,128)} async-done(((f32[1024,128]{0,1:T(8,128)}), f32[128,128]{0,1:T(8,128)}) %reduce-scatter.5.cloned.1.call-update) | async-done | bytes 65552 | tf_op jit(solution)/shard_map/while/body/eval_jaxpr/reduce_scatter | solution.py:46
  236.3 10.4 %all_gather.8 = bf16[1024,128]{0,1:T(8,128)(2,1)S(1)} all-gather(bf16[128,128]{0,1:T(8,128)(2,1)S(1)} %get-tuple-element.271), channel_id=1, replica_groups=mesh['panel'=4,'rows'=8] {'rows'}, dimensions={0}, use_global_device_ids=true | all-gather | bytes 294912 | tf_op jit(solution)/shard_map/while/body/eval_jaxpr/all_gather | solution.py:47
  254.8 4.3 collective-permute-done
  265.0 31.6 %reduce-scatter.5.cloned.1.call-done = f32[128,128]{0,1:T(8,128)} async-done(((f32[1024,128]{0,1:T(8,128)}), f32[128,128]{0,1:T(8,128)}) %reduce-scatter.5.cloned.1.call-update) | async-done | bytes 65552 | tf_op jit(solution)/shard_map/while/body/eval_jaxpr/reduce_scatter | solution.py:46
  297.5 10.4 %all_gather.8 = bf16[1024,128]{0,1:T(8,128)(2,1)S(1)} all-gather(bf16[128,128]{0,1:T(8,128)(2,1)S(1)} %get-tuple-element.271), channel_id=1, replica_groups=mesh['panel'=4,'rows'=8] {'rows'}, dimensions={0}, use_global_device_ids=true | all-gather | bytes 294912 | tf_op jit(solution)/shard_map/while/body/eval_jaxpr/all_gather | solution.py:47
  316.0 4.4 collective-permute-done
  326.2 31.6 %reduce-scatter.5.cloned.1.call-done = f32[128,128]{0,1:T(8,128)} async-done(((f32[1024,128]{0,1:T(8,128)}), f32[128,128]{0,1:T(8,128)}) %reduce-scatter.5.cloned.1.call-update) | async-done | bytes 65552 | tf_op jit(solution)/shard_map/while/body/eval_jaxpr/reduce_scatter | solution.py:46
  358.8 10.4 %all_gather.8 = bf16[1024,128]{0,1:T(8,128)(2,1)S(1)} all-gather(bf16[128,128]{0,1:T(8,128)(2,1)S(1)} %get-tuple-element.271), channel_id=1, replica_groups=mesh['panel'=4,'rows'=8] {'rows'}, dimensions={0}, use_global_device_ids=true | all-gather | bytes 294912 | tf_op jit(solution)/shard_map/while/body/eval_jaxpr/all_gather | solution.py:47
  377.2 4.3 collective-permute-done
  387.4 31.9 %reduce-scatter.5.cloned.1.call-done = f32[128,128]{0,1:T(8,128)} async-done(((f32[1024,128]{0,1:T(8,128)}), f32[128,128]{0,1:T(8,128)}) %reduce-scatter.5.cloned.1.call-update) | async-done | bytes 65552 | tf_op jit(solution)/shard_map/while/body/eval_jaxpr/reduce_scatter | solution.py:46
  420.3 10.4 %all_gather.8 = bf16[1024,128]{0,1:T(8,128)(2,1)S(1)} all-gather(bf16[128,128]{0,1:T(8,128)(2,1)S(1)} %get-tuple-element.271), channel_id=1, replica_groups=mesh['panel'=4,'rows'=8] {'rows'}, dimensions={0}, use_global_device_ids=true | all-gather | bytes 294912 | tf_op jit(solution)/shard_map/while/body/eval_jaxpr/all_gather | solution.py:47
  438.7 4.3 collective-permute-done
  443.0 3.3 fusion.7
  446.5 25.6 %reduce-scatter.3.cloned.1.call-done = f32[1,512,128]{1,2,0:T(8,128)} async-done(((f32[4,512,128]{1,2,0:T(8,128)}), f32[1,512,128]{1,2,0:T(8,128)}) %reduce-scatter.3.cloned.1.call-update) | async-done | bytes 262160 | tf_op jit(solution)/shard_map/reduce_scatter | solution.py:73
  (113 shorter events, 110.3 us)
Async XLA Ops:
  8.0 1.6 copy-start
  12.7 38.5 %reduce-scatter.5.cloned.1.call-start = ((), (), s32[]{:S(2)}) async-start(), calls=%async_computation.3 | async-start | bytes 589824 | tf_op jit(solution)/shard_map/while/body/eval_jaxpr/reduce_scatter | solution.py:46
  65.0 9.9 %collective-permute-start = (f32[512,128]{0,1:T(8,128)}, f32[512,128]{0,1:T(8,128)}, u32[]{:S(2)}, u32[]{:S(2)}) collective-permute-start(f32[512,128]{0,1:T(8,128)} %fusion.26), channel_id=1, source_target_pairs={{0,8},{8,16},{16,24},{1,9},{9,17},{17,25},{2,10},{10,18},{18,26},{... | collective-permute-start | bytes 786440 | tf_op jit(solution)/shard_map/while/body/eval_jaxpr/ppermute | solution.py:10
  74.9 37.8 %reduce-scatter.5.cloned.1.call-start = ((), (), s32[]{:S(2)}) async-start(), calls=%async_computation.3 | async-start | bytes 589824 | tf_op jit(solution)/shard_map/while/body/eval_jaxpr/reduce_scatter | solution.py:46
  126.5 9.9 %collective-permute-start = (f32[512,128]{0,1:T(8,128)}, f32[512,128]{0,1:T(8,128)}, u32[]{:S(2)}, u32[]{:S(2)}) collective-permute-start(f32[512,128]{0,1:T(8,128)} %fusion.26), channel_id=1, source_target_pairs={{0,8},{8,16},{16,24},{1,9},{9,17},{17,25},{2,10},{10,18},{18,26},{... | collective-permute-start | bytes 786440 | tf_op jit(solution)/shard_map/while/body/eval_jaxpr/ppermute | solution.py:10
  136.4 37.8 %reduce-scatter.5.cloned.1.call-start = ((), (), s32[]{:S(2)}) async-start(), calls=%async_computation.3 | async-start | bytes 589824 | tf_op jit(solution)/shard_map/while/body/eval_jaxpr/reduce_scatter | solution.py:46
  188.0 9.9 %collective-permute-start = (f32[512,128]{0,1:T(8,128)}, f32[512,128]{0,1:T(8,128)}, u32[]{:S(2)}, u32[]{:S(2)}) collective-permute-start(f32[512,128]{0,1:T(8,128)} %fusion.26), channel_id=1, source_target_pairs={{0,8},{8,16},{16,24},{1,9},{9,17},{17,25},{2,10},{10,18},{18,26},{... | collective-permute-start | bytes 786440 | tf_op jit(solution)/shard_map/while/body/eval_jaxpr/ppermute | solution.py:10
  197.9 37.5 %reduce-scatter.5.cloned.1.call-start = ((), (), s32[]{:S(2)}) async-start(), calls=%async_computation.3 | async-start | bytes 589824 | tf_op jit(solution)/shard_map/while/body/eval_jaxpr/reduce_scatter | solution.py:46
  249.2 9.9 %collective-permute-start = (f32[512,128]{0,1:T(8,128)}, f32[512,128]{0,1:T(8,128)}, u32[]{:S(2)}, u32[]{:S(2)}) collective-permute-start(f32[512,128]{0,1:T(8,128)} %fusion.26), channel_id=1, source_target_pairs={{0,8},{8,16},{16,24},{1,9},{9,17},{17,25},{2,10},{10,18},{18,26},{... | collective-permute-start | bytes 786440 | tf_op jit(solution)/shard_map/while/body/eval_jaxpr/ppermute | solution.py:10
  259.1 37.5 %reduce-scatter.5.cloned.1.call-start = ((), (), s32[]{:S(2)}) async-start(), calls=%async_computation.3 | async-start | bytes 589824 | tf_op jit(solution)/shard_map/while/body/eval_jaxpr/reduce_scatter | solution.py:46
  310.4 9.9 %collective-permute-start = (f32[512,128]{0,1:T(8,128)}, f32[512,128]{0,1:T(8,128)}, u32[]{:S(2)}, u32[]{:S(2)}) collective-permute-start(f32[512,128]{0,1:T(8,128)} %fusion.26), channel_id=1, source_target_pairs={{0,8},{8,16},{16,24},{1,9},{9,17},{17,25},{2,10},{10,18},{18,26},{... | collective-permute-start | bytes 786440 | tf_op jit(solution)/shard_map/while/body/eval_jaxpr/ppermute | solution.py:10
  320.3 37.5 %reduce-scatter.5.cloned.1.call-start = ((), (), s32[]{:S(2)}) async-start(), calls=%async_computation.3 | async-start | bytes 589824 | tf_op jit(solution)/shard_map/while/body/eval_jaxpr/reduce_scatter | solution.py:46
  371.6 9.9 %collective-permute-start = (f32[512,128]{0,1:T(8,128)}, f32[512,128]{0,1:T(8,128)}, u32[]{:S(2)}, u32[]{:S(2)}) collective-permute-start(f32[512,128]{0,1:T(8,128)} %fusion.26), channel_id=1, source_target_pairs={{0,8},{8,16},{16,24},{1,9},{9,17},{17,25},{2,10},{10,18},{18,26},{... | collective-permute-start | bytes 786440 | tf_op jit(solution)/shard_map/while/body/eval_jaxpr/ppermute | solution.py:10
  381.5 37.8 %reduce-scatter.5.cloned.1.call-start = ((), (), s32[]{:S(2)}) async-start(), calls=%async_computation.3 | async-start | bytes 589824 | tf_op jit(solution)/shard_map/while/body/eval_jaxpr/reduce_scatter | solution.py:46
  433.1 9.9 %collective-permute-start = (f32[512,128]{0,1:T(8,128)}, f32[512,128]{0,1:T(8,128)}, u32[]{:S(2)}, u32[]{:S(2)}) collective-permute-start(f32[512,128]{0,1:T(8,128)} %fusion.26), channel_id=1, source_target_pairs={{0,8},{8,16},{16,24},{1,9},{9,17},{17,25},{2,10},{10,18},{18,26},{... | collective-permute-start | bytes 786440 | tf_op jit(solution)/shard_map/while/body/eval_jaxpr/ppermute | solution.py:10
  443.0 29.2 %reduce-scatter.3.cloned.1.call-start = ((), (), s32[]{:S(2)}) async-start(), calls=%async_computation.2 | async-start | bytes 1310720 | tf_op jit(solution)/shard_map/reduce_scatter | solution.py:73
  443.0 3.4 copy-start.1
Sparse Core Ops, SparseCore 0:
  16.5 34.6 reduce-scatter.4
  78.8 33.9 reduce-scatter.4
  140.3 33.9 reduce-scatter.4
  201.5 33.9 reduce-scatter.4
  262.7 33.9 reduce-scatter.4
  323.9 33.9 reduce-scatter.4
  385.4 33.9 reduce-scatter.4
Sparse Core Ops, SparseCore 1:
  446.5 25.6 reduce-scatter.2
where the time goes:
time: 487 us; the launch traced here: 481 us
  waiting for transfers between devices  279 us (57%)
  blocking collectives  72.8 us (15%)
  matrix products  36.2 us (7%)
  local copies, waits for them, and re-layouts  35.3 us (7%)
  starting transfers between devices  21.8 us (4%)
  other arithmetic  20.3 us (4%)
  between operations  15.5 us (3%)
    reduce_scatter x7, waiting for transfers between devices, advance(): lax.psum_scatter(partial_value, 'rows', scatter_dimension=0, tiled=True)  223 us
    all_gather x7, blocking collectives, advance(): lax.all_gather(own_rows.astype(jnp.bfloat16), 'rows', axis=0, tiled=True)  72.8 us
    ppermute x7, waiting for transfers between devices, shifted(): return lax.ppermute(block, axis, route)  30.4 us
    reduce_scatter x1, waiting for transfers between devices, per_device(): lax.psum_scatter(tall_terms, 'panel', scatter_dimension=0, tiled=True)  25.6 us
    ppermute x7, starting transfers between devices, shifted(): return lax.ppermute(block, axis, route)  21.8 us
    dot_general x7, matrix products, advance(): update = jnp.dot(coupling_here, solved, preferred_element_type=jnp.float32)  17.2 us
    dot_general x7, matrix products, advance(): jnp.dot(inverse_cols, reduced, preferred_element_type=jnp.float32)  15.6 us
    dynamic_update_slice x7, other arithmetic, advance(): lax.dynamic_update_index_in_dim(stored, jnp.where(active, solved, earlier...  12 us
  transfers between devices with their start and end apart: 15, of which 15 were waited for; matrix products, arithmetic and copies ran while one was open for 7% of the time, Pallas kernels for 0%

commit v1 on v0

--- a/solution.py
+++ b/solution.py
@@ -1,7 +1,323 @@
+import functools
+
 import jax
 import jax.numpy as jnp
 from jax import lax
+from jax.experimental import pallas as pl
+from jax.experimental.pallas import tpu as pltpu
 from jax.sharding import PartitionSpec as P
+
+MESH = pl.DeviceIdType.MESH
+CORES = 2
+
+
+def chain_kernel(
+    panels, rhs_ref, tall_rhs_ref, inverse_ref, coupling_ref, tall_ref, mask_ref,
+    sol_ref, res_ref,
+    inv, cpl, tal, msk, rbuf, tbuf, obuf, xs, xf, ysend, ybuf,
+    load_sem, sib_send, sib_recv, first_send, r_sem, t_sem, relay_send, up_send,
+    side_send, sol_send, sol_recv, y_send, y_recv,
+):
+    p = lax.axis_index("panel")
+    r = lax.axis_index("rows")
+    c = lax.rem(r, CORES)
+    j = lax.div(r, CORES)
+    sib = r + 1 - 2 * c
+    batches, half, _ = rhs_ref.shape
+    chips = panels
+    steps = batches // CORES
+    own_rows = sol_ref.shape[1]
+    blocks = mask_ref.shape[0]
+    last = panels - 1
+    chain = j > p
+    feeds_next = j == p + 1
+    relays = jnp.logical_and(j == p, p > 0)
+    first = jnp.logical_and(p == 0, j == 0)
+    next_p = jnp.minimum(p + 1, last)
+
+    def send(src, dst, ssem, rsem, panel, row):
+        return pltpu.make_async_remote_copy(
+            src_ref=src, dst_ref=dst, send_sem=ssem, recv_sem=rsem,
+            device_id=(panel, row), device_id_type=MESH,
+        )
+
+    load_inv = pltpu.make_async_copy(inverse_ref, inv, load_sem.at[0])
+    load_cpl = pltpu.make_async_copy(coupling_ref, cpl.at[c], load_sem.at[1])
+    load_tal = pltpu.make_async_copy(tall_ref, tal.at[c], load_sem.at[2])
+    load_msk = pltpu.make_async_copy(mask_ref, msk.at[c], load_sem.at[3])
+    for load in (load_inv, load_cpl, load_tal, load_msk):
+        load.start()
+
+    def own_rhs(s, into, sem):
+        return pltpu.make_async_copy(rhs_ref.at[CORES * s + c], into.at[s, c], sem.at[s, c])
+
+    @pl.when(first)
+    def _():
+        for s in range(steps):
+            own_rhs(s, rbuf, r_sem).start()
+
+    @pl.when(jnp.logical_and(p == 0, j > 0))
+    def _():
+        for s in range(steps):
+            own_rhs(s, tbuf, t_sem).start()
+
+    barrier = pltpu.get_barrier_semaphore()
+    for q in range(panels):
+        for k in range(CORES):
+            @pl.when(jnp.logical_or(q != p, k != c))
+            def _():
+                pl.semaphore_signal(barrier, inc=1, device_id=(q, CORES * j + k), device_id_type=MESH)
+    for i in range(chips):
+        for k in range(CORES):
+            @pl.when(i != j)
+            def _():
+                pl.semaphore_signal(barrier, inc=1, device_id=(p, CORES * i + k), device_id_type=MESH)
+    side_chip = lax.rem(p + 2, chips)
+    gets_side = jnp.logical_and(p > 0, j == lax.rem(p + 1, chips))
+
+    @pl.when(feeds_next)
+    def _():
+        pl.semaphore_signal(barrier, inc=1, device_id=(next_p, CORES * side_chip + c), device_id_type=MESH)
+
+    @pl.when(gets_side)
+    def _():
+        pl.semaphore_signal(barrier, inc=1, device_id=(jnp.maximum(p - 1, 0), CORES * p + c), device_id_type=MESH)
+
+    pl.semaphore_wait(
+        barrier,
+        CORES * panels - 1 + CORES * (chips - 1) + feeds_next.astype(jnp.int32) + gets_side.astype(jnp.int32),
+    )
+
+    def first_copies():
+        order = [(s, 1) for s in range(steps)] + [(s, i) for i in range(2, chips) for s in range(steps)]
+        return [
+            send(rhs_ref.at[CORES * s + k], rbuf.at[s, c], first_send.at[s, i, k], r_sem.at[s, c], 0, CORES * i + k)
+            for s, i in order for k in range(CORES)
+        ]
+
+    def rhs_swap(s, into, sem):
+        return send(rhs_ref.at[CORES * s + 1 - c], into.at[s, c], sib_send.at[3 + s], sem.at[s, c], p, sib)
+
+    @pl.when(first)
+    def _():
+        for copy in first_copies():
+            copy.start()
+        for s in range(steps):
+            rhs_swap(s, rbuf, r_sem).start()
+
+    @pl.when(jnp.logical_and(p == 0, j > 0))
+    def _():
+        for s in range(steps):
+            rhs_swap(s, tbuf, t_sem).start()
+
+    swap_cpl = send(coupling_ref, cpl.at[c], sib_send.at[0], sib_recv.at[0], p, sib)
+    swap_tal = send(tall_ref, tal.at[c], sib_send.at[1], sib_recv.at[1], p, sib)
+    swap_msk = send(mask_ref, msk.at[c], sib_send.at[2], sib_recv.at[2], p, sib)
+    for swap in (swap_cpl, swap_msk, swap_tal):
+        swap.start()
+
+    def arrived(ref, sem):
+        pltpu.make_async_copy(ref, ref, sem).wait()
+
+    def relay(s, h, n):
+        chip = lax.rem(p + 2 + n, chips)
+        return send(rbuf.at[s, h], rbuf.at[s, h], relay_send.at[s, h, n], r_sem.at[s, h], p, CORES * chip + c)
+
+    def side(s, h):
+        return send(obuf.at[s, h], rbuf.at[s, h], side_send.at[s, h], r_sem.at[s, h], next_p, CORES * side_chip + c)
+
+    def up(s, h, into, sem):
+        return send(obuf.at[s, h], into.at[s, h], up_send.at[s, h], sem.at[s, h], next_p, r)
+
+    def sol_copy(s):
+        return send(
+            xf.at[s, pl.ds(pl.multiple_of(sib * own_rows, own_rows), own_rows)],
+            sol_ref.at[CORES * s + c], sol_send.at[s], sol_recv.at[s], p, sib,
+        )
+
+    def y_copy(s, h):
+        return send(ysend.at[s, h], ybuf.at[p], y_send.at[s, h], y_recv.at[p], CORES * s + c, CORES * j + h)
+
+    def y_local(s, h):
+        return jnp.logical_and(CORES * s + c == p, c == h)
+
+    def tall_part(s):
+        for h in range(CORES):
+            prod = jnp.dot(tal[h], xs[s], preferred_element_type=jnp.float32)
+            prod = prod.reshape(blocks, half // blocks, prod.shape[1]) * msk[h][:, 0:1, :]
+            ysend[s, h] = prod.reshape(half, prod.shape[2]).astype(jnp.bfloat16)
+
+            @pl.when(jnp.logical_not(y_local(s, h)))
+            def _():
+                y_copy(s, h).start()
+
+            @pl.when(y_local(s, h))
+            def _():
+                ybuf[p] = ysend[s, h]
+
+    load_inv.wait()
+    for s in range(steps):
+        for h in range(CORES):
+            arrived(rbuf.at[s, h], r_sem.at[s, h])
+
+            @pl.when(relays)
+            def _():
+                for n in range(chips - 2):
+                    relay(s, h, n).start()
+
+        full = rbuf[s].reshape(inv.shape[1], rbuf.shape[3])
+        for h in range(CORES):
+            x = jnp.dot(inv[h * half:(h + 1) * half], full, preferred_element_type=jnp.float32)
+            xf[s, h * half:(h + 1) * half] = x
+            xs[s, h * half:(h + 1) * half] = x.astype(jnp.bfloat16)
+
+        if s == 0:
+            load_cpl.wait()
+            swap_cpl.wait_recv()
+
+        @pl.when(chain)
+        def _():
+            for h in range(CORES):
+                arrived(tbuf.at[s, h], t_sem.at[s, h])
+                update = jnp.dot(cpl[h], xs[s], preferred_element_type=jnp.float32)
+                obuf[s, h] = (tbuf[s, h].astype(jnp.float32) - update).astype(jnp.bfloat16)
+
+                @pl.when(feeds_next)
+                def _():
+                    side(s, h).start()
+                    up(s, h, rbuf, r_sem).start()
+
+                @pl.when(jnp.logical_not(feeds_next))
+                def _():
+                    up(s, h, tbuf, t_sem).start()
+
+        if s == 0:
+            load_tal.wait()
+            load_msk.wait()
+            swap_tal.wait_recv()
+            swap_msk.wait_recv()
+
+        sol_ref[CORES * s + c] = xf[s, pl.ds(pl.multiple_of(r * own_rows, own_rows), own_rows)]
+        sol_copy(s).start()
+
+        @pl.when(jnp.logical_not(chain))
+        def _():
+            tall_part(s)
+
+    @pl.when(chain)
+    def _():
+        for s in range(steps):
+            tall_part(s)
+
+    total = tall_rhs_ref[...].astype(jnp.float32)
+    for q in range(panels):
+        @pl.when(jnp.logical_not(jnp.logical_and(q == p, c == lax.rem(p, CORES))))
+        def _():
+            arrived(ybuf.at[q], y_recv.at[q])
+    for q in range(panels):
+        total = total - ybuf[q].astype(jnp.float32)
+    res_ref[...] = total
+
+    @pl.when(first)
+    def _():
+        for copy in first_copies():
+            copy.wait_send()
+        for s in range(steps):
+            rhs_swap(s, rbuf, r_sem).wait_send()
+
+    @pl.when(jnp.logical_and(p == 0, j > 0))
+    def _():
+        for s in range(steps):
+            rhs_swap(s, tbuf, t_sem).wait_send()
+
+    for swap in (swap_cpl, swap_msk, swap_tal):
+        swap.wait_send()
+    for s in range(steps):
+        sol_copy(s).wait_send()
+        arrived(sol_ref.at[CORES * s + 1 - c], sol_recv.at[s])
+        for h in range(CORES):
+            @pl.when(relays)
+            def _():
+                for n in range(chips - 2):
+                    relay(s, h, n).wait_send()
+
+            @pl.when(feeds_next)
+            def _():
+                side(s, h).wait_send()
+                up(s, h, rbuf, r_sem).wait_send()
+
+            @pl.when(jnp.logical_and(chain, jnp.logical_not(feeds_next)))
+            def _():
+                up(s, h, tbuf, t_sem).wait_send()
+
+            @pl.when(jnp.logical_not(y_local(s, h)))
+            def _():
+                y_copy(s, h).wait_send()
+
+
+def chained(rhs_diag, rhs_tall, diag_inverse, coupling, tall_blocks, sparsity):
+    panels = lax.axis_size("panel")
+    batches, half, columns = rhs_diag.shape
+    width = diag_inverse.shape[1]
+    own_rows = width // lax.axis_size("rows")
+    blocks, block_rows = tall_blocks.shape[1:3]
+    tall_rows = blocks * block_rows
+    steps = batches // CORES
+    mask = jnp.broadcast_to(sparsity[:, 0].astype(jnp.float32)[:, None, None], (blocks, 8, columns))
+    anywhere = pl.BlockSpec(memory_space=pl.ANY)
+    inside = pl.BlockSpec(memory_space=pltpu.VMEM)
+    bf16, f32 = jnp.bfloat16, jnp.float32
+    dma = pltpu.SemaphoreType.DMA
+    sol, res = pl.pallas_call(
+        functools.partial(chain_kernel, panels),
+        out_shape=(
+            jax.ShapeDtypeStruct((batches, own_rows, columns), f32),
+            jax.ShapeDtypeStruct((tall_rows, columns), f32),
+        ),
+        in_specs=[anywhere, inside, anywhere, anywhere, anywhere, anywhere],
+        out_specs=(inside, inside),
+        scratch_shapes=[
+            pltpu.VMEM((width, width), bf16),
+            pltpu.VMEM((CORES, half, width), bf16),
+            pltpu.VMEM((CORES, tall_rows, width), bf16),
+            pltpu.VMEM((CORES, blocks, 8, columns), f32),
+            pltpu.VMEM((steps, CORES, half, columns), bf16),
+            pltpu.VMEM((steps, CORES, half, columns), bf16),
+            pltpu.VMEM((steps, CORES, half, columns), bf16),
+            pltpu.VMEM((steps, width, columns), bf16),
+            pltpu.VMEM((steps, width, columns), f32),
+            pltpu.VMEM((steps, CORES, tall_rows, columns), bf16),
+            pltpu.VMEM((panels, tall_rows, columns), bf16),
+            dma((4,)),
+            dma((3 + steps,)),
+            dma((3,)),
+            dma((steps, panels, CORES)),
+            dma((steps, CORES)),
+            dma((steps, CORES)),
+            dma((steps, CORES, max(panels - 2, 1))),
+            dma((steps, CORES)),
+            dma((steps, CORES)),
+            dma((steps,)),
+            dma((steps,)),
+            dma((steps, CORES)),
+            dma((panels,)),
+        ],
+        compiler_params=pltpu.CompilerParams(
+            collective_id=0, has_side_effects=True, vmem_limit_bytes=48 * 1024 * 1024
+        ),
+    )(rhs_diag, rhs_tall[0], diag_inverse[0], coupling[0], tall_blocks[0].reshape(tall_rows, width), mask)
+    return sol[None], res[None]
+
+
+def fits_chain(mesh, rhs_diag, rhs_tall, diag_inverse, coupling, tall_blocks):
+    panels, rows = mesh.shape["panel"], mesh.shape["rows"]
+    return (
+        rows == CORES * panels
+        and rhs_diag.shape[1] == panels * diag_inverse.shape[1]
+        and rhs_diag.shape[0] == panels
+        and panels % CORES == 0
+        and tall_blocks.shape[1] * tall_blocks.shape[2] == rhs_diag.shape[1]
+    )
 
 
 def shifted(block, axis, distance):
@@ -84,10 +400,15 @@
         P("panel", "rows", None, None),
         P("rows", "panel"),
     )
-    return jax.shard_map(
-        per_device,
-        mesh=mesh,
-        in_specs=placed,
-        out_specs=(P("panel", None, "rows", None), P("panel", "rows", None)),
-        check_vma=False,
-    )
+
+    def run(*arrays):
+        body = chained if fits_chain(mesh, *arrays[:5]) else per_device
+        return jax.shard_map(
+            body,
+            mesh=mesh,
+            in_specs=placed,
+            out_specs=(P("panel", None, "rows", None), P("panel", "rows", None)),
+            check_vma=False,
+        )(*arrays)
+
+    return run

time: 487 us -> 85.4 us (0.18)
  the two profiles are of different devices: /device:TPU:17 before, /device:TPU:21 now
where the time goes in v1:
time: 85.4 us; the launch traced here: 85.1 us
  Pallas kernels  76.3 us (89%)
  local copies, waits for them, and re-layouts  7.47 us (9%)
    pallas_call x1, Pallas kernels, chained(): pl.pallas_call(functools.partial(chain_kernel, panels), out_shape=(jax.Sh...  76.3 us
    unnamed x12, local copies, waits for them, and re-layouts  7.39 us

profile of v1, /device:TPU:21, one launch (start us, length us, event | category | flops | bytes accessed | tf_op | source)
XLA Modules:
  0.0 85.1 jit_solution(18283369295079291241)
XLA Ops:
  0.6 0.7 convert_bitcast_fusion
  1.3 0.1 broadcast_in_dim.12.mask_ref
  1.4 0.0 copy-start
  1.4 1.6 %copy-done = bf16[1,1024,1024]{2,1,0:T(8,128)(2,1)S(1)} copy-done((bf16[1,1024,1024]{2,1,0:T(8,128)(2,1)S(1)}, bf16[1,1024,1024]{2,1,0:T(8,128)(2,1)}, u32[]{:S(2)}) %copy-start) | copy-done | bytes 2097176
  3.0 0.0 copy-start.1
  3.0 1.2 %copy-done.1 = bf16[1,512,1024]{2,1,0:T(8,128)(2,1)S(1)} copy-done((bf16[1,512,1024]{2,1,0:T(8,128)(2,1)S(1)}, bf16[1,512,1024]{2,1,0:T(8,128)(2,1)}, u32[]{:S(2)}) %copy-start.1) | copy-done | bytes 1048600
  4.2 0.0 copy-start.2
  4.2 1.2 %copy-done.2 = bf16[1,4,128,1024]{3,2,1,0:T(8,128)(2,1)S(1)} copy-done((bf16[1,4,128,1024]{3,2,1,0:T(8,128)(2,1)S(1)}, bf16[1,4,128,1024]{3,2,1,0:T(8,128)(2,1)}, u32[]{:S(2)}) %copy-start.2) | copy-done | bytes 1048600
  5.4 0.0 copy-start.3
  5.4 1.0 %copy-done.3 = bf16[4,512,128]{2,1,0:T(8,128)(2,1)S(1)} copy-done((bf16[4,512,128]{2,1,0:T(8,128)(2,1)S(1)}, bf16[4,512,128]{2,1,0:T(8,128)(2,1)}, u32[]{:S(2)}) %copy-start.3) | copy-done | bytes 524312
  6.4 0.0 copy-start.4
  6.4 0.9 %copy-done.4 = bf16[1,512,128]{2,1,0:T(8,128)(2,1)S(1)} copy-done((bf16[1,512,128]{2,1,0:T(8,128)(2,1)S(1)}, bf16[1,512,128]{2,1,0:T(8,128)(2,1)}, u32[]{:S(2)}) %copy-start.4) | copy-done | bytes 131096
  7.4 76.3 %shard_map.77 = (f32[4,128,128]{2,1,0:T(8,128)S(1)}, f32[512,128]{1,0:T(8,128)S(1)}) custom-call(bf16[4,512,128]{2,1,0:T(8,128)(2,1)S(1)} %copy-done.3, bf16[512,128]{1,0:T(8,128)(2,1)S(1)} %bitcast.13, bf16[1024,1024]{1,0:T(8,128)(2,1)S(1)} %bitcast.8, bf16[512,1024]{1,0:T(8,128)(2,1)S(1)} %bitcast.9, bf16[512,1024]{1,0:T(8,128)(2,1)S(1)} %bitcast.10, ...), custom_call_target="tpu_custom_call" | custom-call | tf_op jit(solution)/shard_map/pallas_call | solution.py:271
  83.7 0.7 copy.10
  84.4 0.7 copy.11
Async XLA Ops:
  1.4 1.6 %copy-start = (bf16[1,1024,1024]{2,1,0:T(8,128)(2,1)S(1)}, bf16[1,1024,1024]{2,1,0:T(8,128)(2,1)}, u32[]{:S(2)}) copy-start(bf16[1,1024,1024]{2,1,0:T(8,128)(2,1)} %param.8) | copy-start | bytes 6291460
  3.0 1.2 %copy-start.1 = (bf16[1,512,1024]{2,1,0:T(8,128)(2,1)S(1)}, bf16[1,512,1024]{2,1,0:T(8,128)(2,1)}, u32[]{:S(2)}) copy-start(bf16[1,512,1024]{2,1,0:T(8,128)(2,1)} %param.9) | copy-start | bytes 3145732
  4.2 1.2 %copy-start.2 = (bf16[1,4,128,1024]{3,2,1,0:T(8,128)(2,1)S(1)}, bf16[1,4,128,1024]{3,2,1,0:T(8,128)(2,1)}, u32[]{:S(2)}) copy-start(bf16[1,4,128,1024]{3,2,1,0:T(8,128)(2,1)} %param.10) | copy-start | bytes 3145732
  5.4 1.0 %copy-start.3 = (bf16[4,512,128]{2,1,0:T(8,128)(2,1)S(1)}, bf16[4,512,128]{2,1,0:T(8,128)(2,1)}, u32[]{:S(2)}) copy-start(bf16[4,512,128]{2,1,0:T(8,128)(2,1)} %rhs_ref.1) | copy-start | bytes 1572868
  6.4 0.9 %copy-start.4 = (bf16[1,512,128]{2,1,0:T(8,128)(2,1)S(1)}, bf16[1,512,128]{2,1,0:T(8,128)(2,1)}, u32[]{:S(2)}) copy-start(bf16[1,512,128]{2,1,0:T(8,128)(2,1)} %param.7) | copy-start | bytes 393220

commit v2 on v1

--- a/solution.py
+++ b/solution.py
@@ -14,9 +14,9 @@
 def chain_kernel(
     panels, rhs_ref, tall_rhs_ref, inverse_ref, coupling_ref, tall_ref, mask_ref,
     sol_ref, res_ref,
-    inv, cpl, tal, msk, rbuf, tbuf, obuf, xs, xf, ysend, ybuf,
-    load_sem, sib_send, sib_recv, first_send, r_sem, t_sem, relay_send, up_send,
-    side_send, sol_send, sol_recv, y_send, y_recv,
+    inv, cpl, tal, msk, rhs, rbuf, tbuf, obuf, xs, xf, ysend, ybuf,
+    load_sem, sib_send, sib_recv, swap_send, r_sem, t_sem, relay_send, up_send,
+    sol_send, sol_recv, y_send, y_recv,
 ):
     p = lax.axis_index("panel")
     r = lax.axis_index("rows")
@@ -26,14 +26,20 @@
     batches, half, _ = rhs_ref.shape
     chips = panels
     steps = batches // CORES
+    parts, part_rows = rbuf.shape[1:3]
+    own_parts = parts // CORES
+    levels = chips.bit_length() - 1
     own_rows = sol_ref.shape[1]
     blocks = mask_ref.shape[0]
     last = panels - 1
     chain = j > p
     feeds_next = j == p + 1
-    relays = jnp.logical_and(j == p, p > 0)
+    next_p = jnp.minimum(p + 1, last)
+    next_root = jnp.minimum(p + 2, last)
+    root = jnp.where(p == 0, 0, jnp.minimum(p + 1, last))
+    place = jnp.bitwise_xor(j, root)
     first = jnp.logical_and(p == 0, j == 0)
-    next_p = jnp.minimum(p + 1, last)
+    later = jnp.logical_and(p == 0, j > 0)
 
     def send(src, dst, ssem, rsem, panel, row):
         return pltpu.make_async_remote_copy(
@@ -45,21 +51,28 @@
     load_cpl = pltpu.make_async_copy(coupling_ref, cpl.at[c], load_sem.at[1])
     load_tal = pltpu.make_async_copy(tall_ref, tal.at[c], load_sem.at[2])
     load_msk = pltpu.make_async_copy(mask_ref, msk.at[c], load_sem.at[3])
-    for load in (load_inv, load_cpl, load_tal, load_msk):
+    load_rhs = pltpu.make_async_copy(tall_rhs_ref, rhs, load_sem.at[4])
+
+    def own_rhs(s, i, into, sem):
+        part = c * own_parts + i
+        return pltpu.make_async_copy(
+            rhs_ref.at[CORES * s + c, pl.ds(i * part_rows, part_rows)], into.at[s, part], sem.at[s, part]
+        )
+
+    pieces = [(s, i) for s in range(steps) for i in range(own_parts)]
+
+    @pl.when(first)
+    def _():
+        for s, i in pieces:
+            own_rhs(s, i, rbuf, r_sem).start()
+
+    @pl.when(later)
+    def _():
+        for s, i in pieces:
+            own_rhs(s, i, tbuf, t_sem).start()
+
+    for load in (load_inv, load_cpl, load_tal, load_msk, load_rhs):
         load.start()
-
-    def own_rhs(s, into, sem):
-        return pltpu.make_async_copy(rhs_ref.at[CORES * s + c], into.at[s, c], sem.at[s, c])
-
-    @pl.when(first)
-    def _():
-        for s in range(steps):
-            own_rhs(s, rbuf, r_sem).start()
-
-    @pl.when(jnp.logical_and(p == 0, j > 0))
-    def _():
-        for s in range(steps):
-            own_rhs(s, tbuf, t_sem).start()
 
     barrier = pltpu.get_barrier_semaphore()
     for q in range(panels):
@@ -72,43 +85,38 @@
             @pl.when(i != j)
             def _():
                 pl.semaphore_signal(barrier, inc=1, device_id=(p, CORES * i + k), device_id_type=MESH)
-    side_chip = lax.rem(p + 2, chips)
-    gets_side = jnp.logical_and(p > 0, j == lax.rem(p + 1, chips))
-
-    @pl.when(feeds_next)
-    def _():
-        pl.semaphore_signal(barrier, inc=1, device_id=(next_p, CORES * side_chip + c), device_id_type=MESH)
-
-    @pl.when(gets_side)
+    leaves = jnp.logical_and(feeds_next, next_root != j)
+    enters = jnp.logical_and(jnp.logical_and(p > 0, j == root), root != p)
+
+    @pl.when(leaves)
+    def _():
+        pl.semaphore_signal(barrier, inc=1, device_id=(next_p, CORES * next_root + c), device_id_type=MESH)
+
+    @pl.when(enters)
     def _():
         pl.semaphore_signal(barrier, inc=1, device_id=(jnp.maximum(p - 1, 0), CORES * p + c), device_id_type=MESH)
 
     pl.semaphore_wait(
         barrier,
-        CORES * panels - 1 + CORES * (chips - 1) + feeds_next.astype(jnp.int32) + gets_side.astype(jnp.int32),
-    )
-
-    def first_copies():
-        order = [(s, 1) for s in range(steps)] + [(s, i) for i in range(2, chips) for s in range(steps)]
-        return [
-            send(rhs_ref.at[CORES * s + k], rbuf.at[s, c], first_send.at[s, i, k], r_sem.at[s, c], 0, CORES * i + k)
-            for s, i in order for k in range(CORES)
-        ]
-
-    def rhs_swap(s, into, sem):
-        return send(rhs_ref.at[CORES * s + 1 - c], into.at[s, c], sib_send.at[3 + s], sem.at[s, c], p, sib)
+        CORES * panels - 1 + CORES * (chips - 1) + leaves.astype(jnp.int32) + enters.astype(jnp.int32),
+    )
+
+    def rhs_swap(s, i, into, sem):
+        part = c * own_parts + i
+        return send(
+            rhs_ref.at[CORES * s + 1 - c, pl.ds(i * part_rows, part_rows)], into.at[s, part],
+            swap_send.at[s, i], sem.at[s, part], p, sib,
+        )
 
     @pl.when(first)
     def _():
-        for copy in first_copies():
-            copy.start()
-        for s in range(steps):
-            rhs_swap(s, rbuf, r_sem).start()
-
-    @pl.when(jnp.logical_and(p == 0, j > 0))
-    def _():
-        for s in range(steps):
-            rhs_swap(s, tbuf, t_sem).start()
+        for s, i in pieces:
+            rhs_swap(s, i, rbuf, r_sem).start()
+
+    @pl.when(later)
+    def _():
+        for s, i in pieces:
+            rhs_swap(s, i, tbuf, t_sem).start()
 
     swap_cpl = send(coupling_ref, cpl.at[c], sib_send.at[0], sib_recv.at[0], p, sib)
     swap_tal = send(tall_ref, tal.at[c], sib_send.at[1], sib_recv.at[1], p, sib)
@@ -119,15 +127,24 @@
     def arrived(ref, sem):
         pltpu.make_async_copy(ref, ref, sem).wait()
 
-    def relay(s, h, n):
-        chip = lax.rem(p + 2 + n, chips)
-        return send(rbuf.at[s, h], rbuf.at[s, h], relay_send.at[s, h, n], r_sem.at[s, h], p, CORES * chip + c)
-
-    def side(s, h):
-        return send(obuf.at[s, h], rbuf.at[s, h], side_send.at[s, h], r_sem.at[s, h], next_p, CORES * side_chip + c)
-
-    def up(s, h, into, sem):
-        return send(obuf.at[s, h], into.at[s, h], up_send.at[s, h], sem.at[s, h], next_p, r)
+    def relay(s, part, level):
+        chip = jnp.bitwise_xor(j, 1 << level)
+        return send(
+            rbuf.at[s, part], rbuf.at[s, part], relay_send.at[s, part, level], r_sem.at[s, part],
+            p, CORES * chip + c,
+        )
+
+    def relays(level):
+        return lax.rem(place, 2 << level) == 0
+
+    def ahead(s, part):
+        return send(
+            obuf.at[s, part], rbuf.at[s, part], up_send.at[s, part], r_sem.at[s, part],
+            next_p, CORES * next_root + c,
+        )
+
+    def up(s, part):
+        return send(obuf.at[s, part], tbuf.at[s, part], up_send.at[s, part], t_sem.at[s, part], next_p, r)
 
     def sol_copy(s):
         return send(
@@ -155,16 +172,18 @@
             def _():
                 ybuf[p] = ysend[s, h]
 
-    load_inv.wait()
+    turn = jnp.where(p == 0, c * own_parts, 0)
     for s in range(steps):
-        for h in range(CORES):
-            arrived(rbuf.at[s, h], r_sem.at[s, h])
-
-            @pl.when(relays)
-            def _():
-                for n in range(chips - 2):
-                    relay(s, h, n).start()
-
+        for i in range(parts):
+            part = lax.rem(i + turn, parts)
+            arrived(rbuf.at[s, part], r_sem.at[s, part])
+            for level in range(levels):
+                @pl.when(relays(level))
+                def _():
+                    relay(s, part, level).start()
+
+        if s == 0:
+            load_inv.wait()
         full = rbuf[s].reshape(inv.shape[1], rbuf.shape[3])
         for h in range(CORES):
             x = jnp.dot(inv[h * half:(h + 1) * half], full, preferred_element_type=jnp.float32)
@@ -177,19 +196,21 @@
 
         @pl.when(chain)
         def _():
-            for h in range(CORES):
-                arrived(tbuf.at[s, h], t_sem.at[s, h])
-                update = jnp.dot(cpl[h], xs[s], preferred_element_type=jnp.float32)
-                obuf[s, h] = (tbuf[s, h].astype(jnp.float32) - update).astype(jnp.bfloat16)
+            for part in range(parts):
+                h, i = divmod(part, own_parts)
+                arrived(tbuf.at[s, part], t_sem.at[s, part])
+                update = jnp.dot(
+                    cpl[h, i * part_rows:(i + 1) * part_rows], xs[s], preferred_element_type=jnp.float32
+                )
+                obuf[s, part] = (tbuf[s, part].astype(jnp.float32) - update).astype(jnp.bfloat16)
 
                 @pl.when(feeds_next)
                 def _():
-                    side(s, h).start()
-                    up(s, h, rbuf, r_sem).start()
+                    ahead(s, part).start()
 
                 @pl.when(jnp.logical_not(feeds_next))
                 def _():
-                    up(s, h, tbuf, t_sem).start()
+                    up(s, part).start()
 
         if s == 0:
             load_tal.wait()
@@ -209,7 +230,8 @@
         for s in range(steps):
             tall_part(s)
 
-    total = tall_rhs_ref[...].astype(jnp.float32)
+    load_rhs.wait()
+    total = rhs[...].astype(jnp.float32)
     for q in range(panels):
         @pl.when(jnp.logical_not(jnp.logical_and(q == p, c == lax.rem(p, CORES))))
         def _():
@@ -218,38 +240,27 @@
         total = total - ybuf[q].astype(jnp.float32)
     res_ref[...] = total
 
-    @pl.when(first)
-    def _():
-        for copy in first_copies():
-            copy.wait_send()
-        for s in range(steps):
-            rhs_swap(s, rbuf, r_sem).wait_send()
-
-    @pl.when(jnp.logical_and(p == 0, j > 0))
-    def _():
-        for s in range(steps):
-            rhs_swap(s, tbuf, t_sem).wait_send()
+    @pl.when(p == 0)
+    def _():
+        for s, i in pieces:
+            rhs_swap(s, i, rbuf, r_sem).wait_send()
 
     for swap in (swap_cpl, swap_msk, swap_tal):
         swap.wait_send()
     for s in range(steps):
         sol_copy(s).wait_send()
         arrived(sol_ref.at[CORES * s + 1 - c], sol_recv.at[s])
+        for part in range(parts):
+            for level in range(levels):
+                @pl.when(relays(level))
+                def _():
+                    relay(s, part, level).wait_send()
+
+            @pl.when(chain)
+            def _():
+                ahead(s, part).wait_send()
+
         for h in range(CORES):
-            @pl.when(relays)
-            def _():
-                for n in range(chips - 2):
-                    relay(s, h, n).wait_send()
-
-            @pl.when(feeds_next)
-            def _():
-                side(s, h).wait_send()
-                up(s, h, rbuf, r_sem).wait_send()
-
-            @pl.when(jnp.logical_and(chain, jnp.logical_not(feeds_next)))
-            def _():
-                up(s, h, tbuf, t_sem).wait_send()
-
             @pl.when(jnp.logical_not(y_local(s, h)))
             def _():
                 y_copy(s, h).wait_send()
@@ -264,7 +275,9 @@
     tall_rows = blocks * block_rows
     steps = batches // CORES
     mask = jnp.broadcast_to(sparsity[:, 0].astype(jnp.float32)[:, None, None], (blocks, 8, columns))
-    anywhere = pl.BlockSpec(memory_space=pl.ANY)
+    parts = 2 * CORES
+    part_rows = width // parts
+    anywhere = pl.BlockSpec(memory_space=pltpu.HBM)
     inside = pl.BlockSpec(memory_space=pltpu.VMEM)
     bf16, f32 = jnp.bfloat16, jnp.float32
     dma = pltpu.SemaphoreType.DMA
@@ -274,36 +287,36 @@
             jax.ShapeDtypeStruct((batches, own_rows, columns), f32),
             jax.ShapeDtypeStruct((tall_rows, columns), f32),
         ),
-        in_specs=[anywhere, inside, anywhere, anywhere, anywhere, anywhere],
+        in_specs=[anywhere] * 6,
         out_specs=(inside, inside),
         scratch_shapes=[
             pltpu.VMEM((width, width), bf16),
             pltpu.VMEM((CORES, half, width), bf16),
             pltpu.VMEM((CORES, tall_rows, width), bf16),
             pltpu.VMEM((CORES, blocks, 8, columns), f32),
-            pltpu.VMEM((steps, CORES, half, columns), bf16),
-            pltpu.VMEM((steps, CORES, half, columns), bf16),
-            pltpu.VMEM((steps, CORES, half, columns), bf16),
+            pltpu.VMEM((tall_rows, columns), bf16),
+            pltpu.VMEM((steps, parts, part_rows, columns), bf16),
+            pltpu.VMEM((steps, parts, part_rows, columns), bf16),
+            pltpu.VMEM((steps, parts, part_rows, columns), bf16),
             pltpu.VMEM((steps, width, columns), bf16),
             pltpu.VMEM((steps, width, columns), f32),
             pltpu.VMEM((steps, CORES, tall_rows, columns), bf16),
             pltpu.VMEM((panels, tall_rows, columns), bf16),
-            dma((4,)),
-            dma((3 + steps,)),
+            dma((5,)),
             dma((3,)),
-            dma((steps, panels, CORES)),
-            dma((steps, CORES)),
-            dma((steps, CORES)),
-            dma((steps, CORES, max(panels - 2, 1))),
-            dma((steps, CORES)),
-            dma((steps, CORES)),
+            dma((3,)),
+            dma((steps, parts // CORES)),
+            dma((steps, parts)),
+            dma((steps, parts)),
+            dma((steps, parts, panels.bit_length())),
+            dma((steps, parts)),
             dma((steps,)),
             dma((steps,)),
             dma((steps, CORES)),
             dma((panels,)),
         ],
         compiler_params=pltpu.CompilerParams(
-            collective_id=0, has_side_effects=True, vmem_limit_bytes=48 * 1024 * 1024
+            collective_id=0, has_side_effects=True, vmem_limit_bytes=67_043_328
         ),
     )(rhs_diag, rhs_tall[0], diag_inverse[0], coupling[0], tall_blocks[0].reshape(tall_rows, width), mask)
     return sol[None], res[None]
@@ -316,6 +329,7 @@
         and rhs_diag.shape[1] == panels * diag_inverse.shape[1]
         and rhs_diag.shape[0] == panels
         and panels % CORES == 0
+        and panels & (panels - 1) == 0
         and tall_blocks.shape[1] * tall_blocks.shape[2] == rhs_diag.shape[1]
     )
 

time: 85.4 us -> 70.3 us (0.82)
  the two profiles are of different devices: /device:TPU:21 before, /device:TPU:17 now
where the time goes in v2:
time: 70.3 us; the launch traced here: 70.1 us
  Pallas kernels  64.8 us (92%)
  local copies, waits for them, and re-layouts  4.02 us (6%)
    pallas_call x1, Pallas kernels, chained(): pl.pallas_call(functools.partial(chain_kernel, panels), out_shape=(jax.Sh...  64.8 us
    unnamed x2, local copies, waits for them, and re-layouts  3.34 us

profile of v2, /device:TPU:17, one launch (start us, length us, event | category | flops | bytes accessed | tf_op | source)
XLA Modules:
  0.0 70.1 jit_solution(11860271391215394361)
XLA Ops:
  0.6 0.7 convert_bitcast_fusion
  1.3 0.7 broadcast_in_dim.12.mask_ref
  2.0 64.8 %shard_map.77 = (f32[4,128,128]{2,1,0:T(8,128)}, f32[512,128]{1,0:T(8,128)}) custom-call(bf16[4,512,128]{2,1,0:T(8,128)(2,1)} %rhs_ref.1, bf16[512,128]{1,0:T(8,128)(2,1)} %bitcast.13, bf16[1024,1024]{1,0:T(8,128)(2,1)} %bitcast.8, bf16[512,1024]{1,0:T(8,128)(2,1)} %bitcast.9, bf16[512,1024]{1,0:T(8,128)(2,1)} %bitcast.10, ...), custom_call_target="tpu_custom_call" | custom-call | tf_op jit(solution)/shard_map/pallas_call | solution.py:284
  66.8 1.7 %copy.10 = f32[1,4,128,128]{3,2,1,0:T(8,128)} copy(f32[1,4,128,128]{3,2,1,0:T(8,128)} %bitcast.12) | data formatting | bytes 524288
  68.5 1.7 %copy.11 = f32[1,512,128]{2,1,0:T(8,128)} copy(f32[1,512,128]{2,1,0:T(8,128)} %bitcast.11) | data formatting | bytes 524288

commit v3 on v2

--- a/solution.py
+++ b/solution.py
@@ -15,7 +15,7 @@
     panels, rhs_ref, tall_rhs_ref, inverse_ref, coupling_ref, tall_ref, mask_ref,
     sol_ref, res_ref,
     inv, cpl, tal, msk, rhs, rbuf, tbuf, obuf, xs, xf, ysend, ybuf,
-    load_sem, sib_send, sib_recv, swap_send, r_sem, t_sem, relay_send, up_send,
+    load_sem, sib_send, sib_recv, swap_send, first_send, r_sem, t_sem, relay_send, up_send,
     sol_send, sol_recv, y_send, y_recv,
 ):
     p = lax.axis_index("panel")
@@ -108,8 +108,19 @@
             swap_send.at[s, i], sem.at[s, part], p, sib,
         )
 
+    def outward(k, level, i):
+        part = c * own_parts + i
+        return send(
+            rhs_ref.at[k, pl.ds(i * part_rows, part_rows)], rbuf.at[k // CORES, part],
+            first_send.at[k, level, i], r_sem.at[k // CORES, part], p, (CORES << level) + k % CORES,
+        )
+
+    outwards = [(k, n, i) for k in range(batches) for n in range(levels) for i in range(own_parts)]
+
     @pl.when(first)
     def _():
+        for k, level, i in outwards:
+            outward(k, level, i).start()
         for s, i in pieces:
             rhs_swap(s, i, rbuf, r_sem).start()
 
@@ -135,7 +146,7 @@
         )
 
     def relays(level):
-        return lax.rem(place, 2 << level) == 0
+        return jnp.logical_and(lax.rem(place, 2 << level) == 0, jnp.logical_not(first))
 
     def ahead(s, part):
         return send(
@@ -172,23 +183,20 @@
             def _():
                 ybuf[p] = ysend[s, h]
 
-    turn = jnp.where(p == 0, c * own_parts, 0)
+    load_inv.wait()
     for s in range(steps):
-        for i in range(parts):
-            part = lax.rem(i + turn, parts)
+        for part in range(parts):
             arrived(rbuf.at[s, part], r_sem.at[s, part])
             for level in range(levels):
                 @pl.when(relays(level))
                 def _():
                     relay(s, part, level).start()
 
-        if s == 0:
-            load_inv.wait()
-        full = rbuf[s].reshape(inv.shape[1], rbuf.shape[3])
-        for h in range(CORES):
-            x = jnp.dot(inv[h * half:(h + 1) * half], full, preferred_element_type=jnp.float32)
-            xf[s, h * half:(h + 1) * half] = x
-            xs[s, h * half:(h + 1) * half] = x.astype(jnp.bfloat16)
+            x = jnp.dot(
+                inv[:, part * part_rows:(part + 1) * part_rows], rbuf[s, part], preferred_element_type=jnp.float32
+            )
+            xf[s] = x if part == 0 else xf[s] + x
+        xs[s] = xf[s].astype(jnp.bfloat16)
 
         if s == 0:
             load_cpl.wait()
@@ -244,6 +252,11 @@
     def _():
         for s, i in pieces:
             rhs_swap(s, i, rbuf, r_sem).wait_send()
+
+    @pl.when(first)
+    def _():
+        for k, level, i in outwards:
+            outward(k, level, i).wait_send()
 
     for swap in (swap_cpl, swap_msk, swap_tal):
         swap.wait_send()
@@ -306,6 +319,7 @@
             dma((3,)),
             dma((3,)),
             dma((steps, parts // CORES)),
+            dma((batches, panels.bit_length(), parts // CORES)),
             dma((steps, parts)),
             dma((steps, parts)),
             dma((steps, parts, panels.bit_length())),

time: 70.3 us -> 67.8 us (0.964)
  Pallas kernels: 64.8 us -> 62.3 us
    pallas_call x1, Pallas kernels: 64.8 us -> 62.3 us  [chained(): pl.pallas_call(functools.partial(chain_kernel, panels), out_shape=(jax.Sh...]
where the time goes in v3:
time: 67.8 us; the launch traced here: 67.6 us
  Pallas kernels  62.3 us (92%)
  local copies, waits for them, and re-layouts  4.02 us (6%)
    pallas_call x1, Pallas kernels, chained(): pl.pallas_call(functools.partial(chain_kernel, panels), out_shape=(jax.Sh...  62.3 us
    unnamed x2, local copies, waits for them, and re-layouts  3.34 us

profile of v3, /device:TPU:17, one launch (start us, length us, event | category | flops | bytes accessed | tf_op | source)
XLA Modules:
  0.0 67.6 jit_solution(1386030634236713191)
XLA Ops:
  0.6 0.7 convert_bitcast_fusion
  1.3 0.7 %broadcast_in_dim.12.mask_ref = f32[4,8,128]{2,1,0:T(8,128)} broadcast(f32[4]{0:T(128)S(1)} %convert_bitcast_fusion), dimensions={0} | broadcast | bytes 16400 | tf_op jit(solution)/shard_map/broadcast_in_dim | solution.py:290
  2.0 62.3 %shard_map.77 = (f32[4,128,128]{2,1,0:T(8,128)}, f32[512,128]{1,0:T(8,128)}) custom-call(bf16[4,512,128]{2,1,0:T(8,128)(2,1)} %rhs_ref.1, bf16[512,128]{1,0:T(8,128)(2,1)} %bitcast.13, bf16[1024,1024]{1,0:T(8,128)(2,1)} %bitcast.8, bf16[512,1024]{1,0:T(8,128)(2,1)} %bitcast.9, bf16[512,1024]{1,0:T(8,128)(2,1)} %bitcast.10, ...), custom_call_target="tpu_custom_call" | custom-call | tf_op jit(solution)/shard_map/pallas_call | solution.py:297
  64.3 1.7 %copy.10 = f32[1,4,128,128]{3,2,1,0:T(8,128)} copy(f32[1,4,128,128]{3,2,1,0:T(8,128)} %bitcast.12) | data formatting | bytes 524288
  66.0 1.7 %copy.11 = f32[1,512,128]{2,1,0:T(8,128)} copy(f32[1,512,128]{2,1,0:T(8,128)} %bitcast.11) | data formatting | bytes 524288

commit v4 on v3

--- a/solution.py
+++ b/solution.py
@@ -12,7 +12,7 @@
 
 
 def chain_kernel(
-    panels, rhs_ref, tall_rhs_ref, inverse_ref, coupling_ref, tall_ref, mask_ref,
+    panels, rhs_ref, tall_rhs_ref, inverse_ref, coupling_ref, tall_ref, flag_ref,
     sol_ref, res_ref,
     inv, cpl, tal, msk, rhs, rbuf, tbuf, obuf, xs, xf, ysend, ybuf,
     load_sem, sib_send, sib_recv, swap_send, first_send, r_sem, t_sem, relay_send, up_send,
@@ -30,7 +30,8 @@
     own_parts = parts // CORES
     levels = chips.bit_length() - 1
     own_rows = sol_ref.shape[1]
-    blocks = mask_ref.shape[0]
+    blocks = flag_ref.shape[0]
+    pair = 2
     last = panels - 1
     chain = j > p
     feeds_next = j == p + 1
@@ -50,8 +51,10 @@
     load_inv = pltpu.make_async_copy(inverse_ref, inv, load_sem.at[0])
     load_cpl = pltpu.make_async_copy(coupling_ref, cpl.at[c], load_sem.at[1])
     load_tal = pltpu.make_async_copy(tall_ref, tal.at[c], load_sem.at[2])
-    load_msk = pltpu.make_async_copy(mask_ref, msk.at[c], load_sem.at[3])
-    load_rhs = pltpu.make_async_copy(tall_rhs_ref, rhs, load_sem.at[4])
+    flags = flag_ref[...].astype(jnp.float32)
+    for b in range(blocks):
+        msk[c, b] = jnp.broadcast_to(flags[b:b + 1, 0:1], msk.shape[2:])
+    load_rhs = pltpu.make_async_copy(tall_rhs_ref, rhs, load_sem.at[3])
 
     def own_rhs(s, i, into, sem):
         part = c * own_parts + i
@@ -71,7 +74,7 @@
         for s, i in pieces:
             own_rhs(s, i, tbuf, t_sem).start()
 
-    for load in (load_inv, load_cpl, load_tal, load_msk, load_rhs):
+    for load in (load_inv, load_cpl, load_tal, load_rhs):
         load.start()
 
     barrier = pltpu.get_barrier_semaphore()
@@ -131,7 +134,7 @@
 
     swap_cpl = send(coupling_ref, cpl.at[c], sib_send.at[0], sib_recv.at[0], p, sib)
     swap_tal = send(tall_ref, tal.at[c], sib_send.at[1], sib_recv.at[1], p, sib)
-    swap_msk = send(mask_ref, msk.at[c], sib_send.at[2], sib_recv.at[2], p, sib)
+    swap_msk = send(msk.at[c], msk.at[c], sib_send.at[2], sib_recv.at[2], p, sib)
     for swap in (swap_cpl, swap_msk, swap_tal):
         swap.start()
 
@@ -192,10 +195,14 @@
                 def _():
                     relay(s, part, level).start()
 
-            x = jnp.dot(
-                inv[:, part * part_rows:(part + 1) * part_rows], rbuf[s, part], preferred_element_type=jnp.float32
-            )
-            xf[s] = x if part == 0 else xf[s] + x
+            if part % pair == pair - 1:
+                start = part + 1 - pair
+                x = jnp.dot(
+                    inv[:, start * part_rows:(part + 1) * part_rows],
+                    rbuf[s, start:part + 1].reshape(pair * part_rows, rbuf.shape[3]),
+                    preferred_element_type=jnp.float32,
+                )
+                xf[s] = x if start == 0 else xf[s] + x
         xs[s] = xf[s].astype(jnp.bfloat16)
 
         if s == 0:
@@ -204,25 +211,29 @@
 
         @pl.when(chain)
         def _():
-            for part in range(parts):
-                h, i = divmod(part, own_parts)
-                arrived(tbuf.at[s, part], t_sem.at[s, part])
+            for start in range(0, parts, pair):
+                h, i = divmod(start, own_parts)
+                both = range(start, start + pair)
+                for part in both:
+                    arrived(tbuf.at[s, part], t_sem.at[s, part])
                 update = jnp.dot(
-                    cpl[h, i * part_rows:(i + 1) * part_rows], xs[s], preferred_element_type=jnp.float32
-                )
-                obuf[s, part] = (tbuf[s, part].astype(jnp.float32) - update).astype(jnp.bfloat16)
+                    cpl[h, i * part_rows:(i + pair) * part_rows], xs[s], preferred_element_type=jnp.float32
+                ).reshape(pair, part_rows, xs.shape[2])
+                for n, part in enumerate(both):
+                    obuf[s, part] = (tbuf[s, part].astype(jnp.float32) - update[n]).astype(jnp.bfloat16)
 
                 @pl.when(feeds_next)
                 def _():
-                    ahead(s, part).start()
+                    for part in both:
+                        ahead(s, part).start()
 
                 @pl.when(jnp.logical_not(feeds_next))
                 def _():
-                    up(s, part).start()
+                    for part in both:
+                        up(s, part).start()
 
         if s == 0:
             load_tal.wait()
-            load_msk.wait()
             swap_tal.wait_recv()
             swap_msk.wait_recv()
 
@@ -287,8 +298,7 @@
     blocks, block_rows = tall_blocks.shape[1:3]
     tall_rows = blocks * block_rows
     steps = batches // CORES
-    mask = jnp.broadcast_to(sparsity[:, 0].astype(jnp.float32)[:, None, None], (blocks, 8, columns))
-    parts = 2 * CORES
+    parts = 4 * CORES
     part_rows = width // parts
     anywhere = pl.BlockSpec(memory_space=pltpu.HBM)
     inside = pl.BlockSpec(memory_space=pltpu.VMEM)
@@ -300,7 +310,7 @@
             jax.ShapeDtypeStruct((batches, own_rows, columns), f32),
             jax.ShapeDtypeStruct((tall_rows, columns), f32),
         ),
-        in_specs=[anywhere] * 6,
+        in_specs=[anywhere] * 5 + [inside],
         out_specs=(inside, inside),
         scratch_shapes=[
             pltpu.VMEM((width, width), bf16),
@@ -315,7 +325,7 @@
             pltpu.VMEM((steps, width, columns), f32),
             pltpu.VMEM((steps, CORES, tall_rows, columns), bf16),
             pltpu.VMEM((panels, tall_rows, columns), bf16),
-            dma((5,)),
+            dma((4,)),
             dma((3,)),
             dma((3,)),
             dma((steps, parts // CORES)),
@@ -332,7 +342,7 @@
         compiler_params=pltpu.CompilerParams(
             collective_id=0, has_side_effects=True, vmem_limit_bytes=67_043_328
         ),
-    )(rhs_diag, rhs_tall[0], diag_inverse[0], coupling[0], tall_blocks[0].reshape(tall_rows, width), mask)
+    )(rhs_diag, rhs_tall[0], diag_inverse[0], coupling[0], tall_blocks[0].reshape(tall_rows, width), sparsity)
     return sol[None], res[None]
 
 

time: 67.8 us -> 68.2 us (level)
    unnamed x2 -> x3, local copies, waits for them, and re-layouts: 3.34 us -> 4.65 us
where the time goes in v4:
time: 68.2 us; the launch traced here: 68 us
  Pallas kernels  62.7 us (92%)
  local copies, waits for them, and re-layouts  4.65 us (7%)
    pallas_call x1, Pallas kernels, chained(): pl.pallas_call(functools.partial(chain_kernel, panels), out_shape=(jax.Sh...  62.7 us
    unnamed x3, local copies, waits for them, and re-layouts  4.65 us

profile of v4, /device:TPU:17, one launch (start us, length us, event | category | flops | bytes accessed | tf_op | source)
XLA Modules:
  0.0 68.0 jit_solution(14367903812463725751)
XLA Ops:
  0.6 1.3 %copy.8.flag_ref = s32[4,1]{1,0:T(4,128)} copy(s32[4,1]{0,1:T(1,128)} %param.11) | data formatting | bytes 32 | tf_op args[5]
  1.9 62.7 %shard_map.77 = (f32[4,128,128]{2,1,0:T(8,128)}, f32[512,128]{1,0:T(8,128)}) custom-call(bf16[4,512,128]{2,1,0:T(8,128)(2,1)} %rhs_ref.1, bf16[512,128]{1,0:T(8,128)(2,1)} %bitcast.11, bf16[1024,1024]{1,0:T(8,128)(2,1)} %bitcast.6, bf16[512,1024]{1,0:T(8,128)(2,1)} %bitcast.7, bf16[512,1024]{1,0:T(8,128)(2,1)} %bitcast.8, s32[4,1]{1,0:T(4,128)} %copy.8.flag_ref), custom_call_target="tpu_custom_call" | custom-call | tf_op jit(solution)/shard_map/pallas_call | solution.py:307
  64.6 1.7 %copy.11 = f32[1,4,128,128]{3,2,1,0:T(8,128)} copy(f32[1,4,128,128]{3,2,1,0:T(8,128)} %bitcast.10) | data formatting | bytes 524288
  66.3 1.7 %copy.12 = f32[1,512,128]{2,1,0:T(8,128)} copy(f32[1,512,128]{2,1,0:T(8,128)} %bitcast.9) | data formatting | bytes 524288

commit v5 on v4

--- a/solution.py
+++ b/solution.py
@@ -31,7 +31,7 @@
     levels = chips.bit_length() - 1
     own_rows = sol_ref.shape[1]
     blocks = flag_ref.shape[0]
-    pair = 2
+    pair = 1
     last = panels - 1
     chain = j > p
     feeds_next = j == p + 1
@@ -298,7 +298,7 @@
     blocks, block_rows = tall_blocks.shape[1:3]
     tall_rows = blocks * block_rows
     steps = batches // CORES
-    parts = 4 * CORES
+    parts = 2 * CORES
     part_rows = width // parts
     anywhere = pl.BlockSpec(memory_space=pltpu.HBM)
     inside = pl.BlockSpec(memory_space=pltpu.VMEM)

time: 68.2 us -> 68.5 us (level)
  no operation moved by 1% of the time
where the time goes in v5:
time: 68.5 us; the launch traced here: 68.3 us
  Pallas kernels  63 us (92%)
  local copies, waits for them, and re-layouts  4.65 us (7%)
    pallas_call x1, Pallas kernels, chained(): pl.pallas_call(functools.partial(chain_kernel, panels), out_shape=(jax.Sh...  63 us
    unnamed x3, local copies, waits for them, and re-layouts  4.65 us

profile of v5, /device:TPU:17, one launch (start us, length us, event | category | flops | bytes accessed | tf_op | source)
XLA Modules:
  0.0 68.3 jit_solution(9299212360094893998)
XLA Ops:
  0.6 1.3 %copy.8.flag_ref = s32[4,1]{1,0:T(4,128)} copy(s32[4,1]{0,1:T(1,128)} %param.11) | data formatting | bytes 32 | tf_op args[5]
  1.9 63.0 %shard_map.77 = (f32[4,128,128]{2,1,0:T(8,128)}, f32[512,128]{1,0:T(8,128)}) custom-call(bf16[4,512,128]{2,1,0:T(8,128)(2,1)} %rhs_ref.1, bf16[512,128]{1,0:T(8,128)(2,1)} %bitcast.11, bf16[1024,1024]{1,0:T(8,128)(2,1)} %bitcast.6, bf16[512,1024]{1,0:T(8,128)(2,1)} %bitcast.7, bf16[512,1024]{1,0:T(8,128)(2,1)} %bitcast.8, s32[4,1]{1,0:T(4,128)} %copy.8.flag_ref), custom_call_target="tpu_custom_call" | custom-call | tf_op jit(solution)/shard_map/pallas_call | solution.py:307
  65.0 1.7 %copy.11 = f32[1,4,128,128]{3,2,1,0:T(8,128)} copy(f32[1,4,128,128]{3,2,1,0:T(8,128)} %bitcast.10) | data formatting | bytes 524288
  66.6 1.7 %copy.12 = f32[1,512,128]{2,1,0:T(8,128)} copy(f32[1,512,128]{2,1,0:T(8,128)} %bitcast.9) | data formatting | bytes 524288
